TPU v7x, 128 devices: a whole 4x4x4 slice. The times are simulated.
128 devices in a mesh: ty: 8 (over x, core), tx: 16 (over y, z).
Axes of the slice: x: 4, y: 4, z: 4, core: 2. Of those that a mesh axis runs over, the one named last changes fastest.
Arguments:
- measured: float32 [8, 16, 32, 128, 128], P('ty', 'tx'), may hold values from 0 to 4
- positions: int32 [8, 16, 32, 2], P('ty', 'tx'), may hold values from 0 to 511, as said below
- owners: int32 [8, 16, 32], P('ty', 'tx'), may hold values from 0 to 127, as said below
- counts: int32 [8, 16], P('ty', 'tx'), may hold values from 16 to 32, as said below
- object_field: float32 [2, 4096, 8192], P(None, 'ty', 'tx'), may hold values from -4 to 4
- probe_field: float32 [2, 128, 128], replicated, may hold values from -6 to 6
Outputs:
- new_object: float32 [2, 4096, 8192], P(None, 'ty', 'tx')
- new_probe: float32 [2, 128, 128], replicated
Inputs may be any that keep to these rules, and one draw needn't show every extreme that they name: `positions`: for a live slot the entry is a cell of the owner's tile: row below 512, column below 512; other slots hold arbitrary cells of a tile. The owner of a live slot is the holding device's own tile or one of the up to eight tiles beside it (diagonals included). From one device at most 2 live slots go to any one other tile, and in every draw some tile receives exactly 2 from each of its eight neighbours. Slots that are not live hold arbitrary owners. `counts`: some device is full (32 live slots) in every draw.
All inputs are finite; a program needn't handle non-finite values.
Results may differ from a plain program's by a relative error of at most 0.0003.
Values sent between devices are 32-bit elements; how exact they have to be, the bound alone decides.
A program may use at most 128 MiB of HBM per device.

v0:
```python
import math
import jax
import jax.numpy as jnp
from jax import lax
from jax.sharding import PartitionSpec as P

M = 128
MOVE = 2
BLK = 8
offset_level = 1.0
floor_level = 1.0
tiny_level = 1e-06


def padded_2(value, sides, width):
    for axis, dim in sides:
        devices, length = (lax.axis_size(axis), value.shape[dim])
        up = [(i, (i + 1) % devices) for i in range(devices - 1)]
        down = [(j, i) for i, j in up]
        last = lax.slice_in_dim(value, length - width, length, axis=dim)
        leading = lax.slice_in_dim(value, 0, width, axis=dim)
        before = lax.ppermute(last, axis, up)
        after = lax.ppermute(leading, axis, down)
        value = jnp.concatenate([before, value, after], axis=dim)
    return value


def from_behind(block, axis, distance):
    devices = range(lax.axis_size(axis))
    route = [(i - distance, i) for i in devices if i - distance in devices]
    return lax.ppermute(block, axis, route)


def dft_tables(length_side):
    row_ids = lax.broadcasted_iota(jnp.int32, (length_side, length_side), 0)
    col_ids = lax.broadcasted_iota(jnp.int32, (length_side, length_side), 1)
    phase = (row_ids * col_ids % length_side).astype(jnp.float32) * (2.0 * math.pi / length_side)
    factor = 1.0 / math.sqrt(length_side)
    return (jnp.cos(phase) * factor, -jnp.sin(phase) * factor)


def transform(real_part, imag_part, cosine_table, sine_table):
    highest = lax.Precision.HIGHEST
    left_real = jnp.einsum("jk,bkl->bjl", cosine_table, real_part, precision=highest) - jnp.einsum(
        "jk,bkl->bjl", sine_table, imag_part, precision=highest
    )
    left_imag = jnp.einsum("jk,bkl->bjl", cosine_table, imag_part, precision=highest) + jnp.einsum(
        "jk,bkl->bjl", sine_table, real_part, precision=highest
    )
    outer_real = jnp.einsum("bjk,kl->bjl", left_real, cosine_table, precision=highest) - jnp.einsum(
        "bjk,kl->bjl", left_imag, sine_table, precision=highest
    )
    outer_imag = jnp.einsum("bjk,kl->bjl", left_real, sine_table, precision=highest) + jnp.einsum(
        "bjk,kl->bjl", left_imag, cosine_table, precision=highest
    )
    return (outer_real, outer_imag)


def pattern_terms(probe_field, patches, measured_block, live_mask, cosine_table, sine_table):
    probe_real = probe_field[0]
    probe_imag = probe_field[1]
    patch_real = patches[:, 0]
    patch_imag = patches[:, 1]
    exit_real = probe_real * patch_real - probe_imag * patch_imag
    exit_imag = probe_real * patch_imag + probe_imag * patch_real
    far_real, far_imag = transform(exit_real, exit_imag, cosine_table, sine_table)
    power = far_real * far_real + far_imag * far_imag
    ratio = 1.0 - measured_block / (power + offset_level)
    chi_real, chi_imag = transform(far_real * ratio, far_imag * ratio, cosine_table, -sine_table)
    chi_real = chi_real * live_mask[:, None, None]
    chi_imag = chi_imag * live_mask[:, None, None]
    object_real = probe_real * chi_real + probe_imag * chi_imag
    object_imag = probe_real * chi_imag - probe_imag * chi_real
    lighting = (probe_real * probe_real + probe_imag * probe_imag)[None] * live_mask[:, None, None]
    spread = jnp.stack([object_real, object_imag, lighting], axis=1)
    grad_real = jnp.sum(patch_real * chi_real + patch_imag * chi_imag, axis=0)
    grad_imag = jnp.sum(patch_real * chi_imag - patch_imag * chi_real, axis=0)
    weight = jnp.sum(
        (patch_real * patch_real + patch_imag * patch_imag) * live_mask[:, None, None], axis=0
    )
    return (spread, grad_real, grad_imag, weight)


def add_patches(accumulated, spread, start_rows, start_cols):
    zero_index = jnp.zeros((), jnp.int32)

    def add_one(patch_id, current):
        row_start = start_rows[patch_id]
        col_start = start_cols[patch_id]
        window = lax.dynamic_slice(current, (zero_index, row_start, col_start), spread.shape[1:])
        return lax.dynamic_update_slice(
            current, window + spread[patch_id], (zero_index, row_start, col_start)
        )

    return lax.fori_loop(0, spread.shape[0], add_one, accumulated)


def offsets(slot_tags, row_here, col_here, grid_cols):
    owner_id = slot_tags[:, 2] - 1
    is_valid = owner_id >= 0
    safe_owner = jnp.maximum(owner_id, 0)
    return (is_valid, safe_owner // grid_cols - row_here, safe_owner % grid_cols - col_here)


def select_slots(chosen, capacity, slot_rows, slot_tags):
    slot_count = chosen.shape[0]
    sort_key = jnp.where(chosen, 0, slot_count) + jnp.arange(slot_count, dtype=jnp.int32)
    picked = jnp.argsort(sort_key)[:capacity]
    kept_mask = jnp.take(chosen, picked)
    return (
        jnp.take(slot_rows, picked, axis=0),
        jnp.where(kept_mask[:, None], jnp.take(slot_tags, picked, axis=0), 0),
    )


def shards(measured, positions, owners, counts, object_field, probe_field):
    tile_rows = object_field.shape[1]
    tile_cols = object_field.shape[2]
    rim_width = M // 2
    grid_cols = lax.axis_size("tx")
    row_here = lax.axis_index("ty")
    col_here = lax.axis_index("tx")
    self_index = row_here * grid_cols + col_here
    padded = padded_2(object_field, (("ty", 1), ("tx", 2)), rim_width)
    own_rows = measured[0, 0]
    slot_ids = jnp.arange(own_rows.shape[0], dtype=jnp.int32)
    slot_alive = slot_ids < counts[0, 0]
    slot_info = jnp.concatenate([positions[0, 0], owners[0, 0][:, None]], axis=1) + 1
    own_tags = jnp.where(slot_alive[:, None], slot_info, 0)
    is_valid, row_offset, col_offset = offsets(own_tags, row_here, col_here, grid_cols)
    piece_rows = [own_rows]
    piece_tags = [own_tags]
    neighbours = [(-1, -1), (-1, 0), (-1, 1), (0, -1), (0, 1), (1, -1), (1, 0), (1, 1)]
    for down_step, right_step in neighbours:
        chosen = is_valid & (row_offset == down_step) & (col_offset == right_step)
        sent_rows, sent_tags = select_slots(chosen, MOVE, own_rows, own_tags)
        if down_step == 0:
            sent_rows, sent_tags = from_behind((sent_rows, sent_tags), "tx", right_step)
        elif right_step == 0:
            sent_rows, sent_tags = from_behind((sent_rows, sent_tags), "ty", down_step)
        else:
            sent_rows, sent_tags = from_behind((sent_rows, sent_tags), "tx", right_step)
            sent_rows, sent_tags = from_behind((sent_rows, sent_tags), "ty", down_step)
        piece_rows.append(sent_rows)
        piece_tags.append(sent_tags)
    all_rows = jnp.concatenate(piece_rows, axis=0)
    all_tags = jnp.concatenate(piece_tags, axis=0)
    valid_all = all_tags[:, 2] - 1 == self_index
    slot_total = all_rows.shape[0]
    slot_index = jnp.arange(slot_total, dtype=jnp.int32)
    slot_order = jnp.argsort(jnp.where(valid_all, 0, slot_total) + slot_index)
    block_turns = (jnp.sum(valid_all.astype(jnp.int32)) + BLK - 1) // BLK
    cosine_table, sine_table = dft_tables(M)
    zero_index = jnp.zeros((), jnp.int32)

    def one_block(block_id, state_carry):
        accumulated, grad_real, grad_imag, weight = state_carry
        picked = lax.dynamic_slice_in_dim(slot_order, block_id * BLK, BLK)
        block_rows = jnp.take(all_rows, picked, axis=0)
        block_tags = jnp.take(all_tags, picked, axis=0)
        live_mask = jnp.take(valid_all, picked).astype(jnp.float32)
        start_rows = jnp.clip(block_tags[:, 0] - 1, 0, tile_rows - 1)
        start_cols = jnp.clip(block_tags[:, 1] - 1, 0, tile_cols - 1)
        patches = jax.vmap(
            lambda row_start, col_start: lax.dynamic_slice(
                padded, (zero_index, row_start, col_start), (2, M, M)
            )
        )(start_rows, start_cols)
        spread, part_real, part_imag, part_weight = pattern_terms(
            probe_field, patches, block_rows, live_mask, cosine_table, sine_table
        )
        accumulated = add_patches(accumulated, spread, start_rows, start_cols)
        return (accumulated, grad_real + part_real, grad_imag + part_imag, weight + part_weight)

    start_state = (
        jnp.zeros((3, tile_rows + M, tile_cols + M), jnp.float32),
        jnp.zeros((M, M), jnp.float32),
        jnp.zeros((M, M), jnp.float32),
        jnp.zeros((M, M), jnp.float32),
    )
    accumulated, grad_real, grad_imag, weight = lax.fori_loop(
        0, block_turns, one_block, start_state
    )
    for direction in (1, -1):
        rim_strip = (
            accumulated[:, tile_rows + rim_width :, :]
            if direction == 1
            else accumulated[:, :rim_width, :]
        )
        arrived = from_behind(rim_strip, "ty", direction)
        if direction == 1:
            accumulated = accumulated.at[:, rim_width : 2 * rim_width, :].add(arrived)
        else:
            accumulated = accumulated.at[:, tile_rows : tile_rows + rim_width, :].add(arrived)
    for direction in (1, -1):
        rim_strip = (
            accumulated[:, :, tile_cols + rim_width :]
            if direction == 1
            else accumulated[:, :, :rim_width]
        )
        arrived = from_behind(rim_strip, "tx", direction)
        if direction == 1:
            accumulated = accumulated.at[:, :, rim_width : 2 * rim_width].add(arrived)
        else:
            accumulated = accumulated.at[:, :, tile_cols : tile_cols + rim_width].add(arrived)
    interior = accumulated[:, rim_width : rim_width + tile_rows, rim_width : rim_width + tile_cols]
    new_object = object_field - interior[:2] / (interior[2] + floor_level)
    summed = lax.psum((grad_real, grad_imag, weight), ("ty", "tx"))
    new_probe = probe_field - jnp.stack([summed[0], summed[1]]) / (summed[2] + tiny_level)
    return (new_object, new_probe)


def solution(mesh):
    placed = (
        P("ty", "tx", None, None, None),
        P("ty", "tx", None, None),
        P("ty", "tx", None),
        P("ty", "tx"),
        P(None, "ty", "tx"),
        P(),
    )
    return jax.shard_map(
        shards, mesh=mesh, in_specs=placed, out_specs=(P(None, "ty", "tx"), P()), check_vma=False
    )
```

profile of v0, /device:TPU:1, one launch (start us, length us, event | category | flops | bytes accessed | tf_op | source)
XLA Modules:
  0.0 1042.0 jit_solution(12287225430988321243)
XLA Ops:
  24.3 4.9 collective-permute-start.3
  36.8 4.0 collective-permute-start.6
  65.8 3.9 collective-permute-start.9
  69.9 4.3 collective-permute-start.10
  74.2 5.3 collective-permute-start.26
  79.6 5.7 collective-permute-start.19
  105.3 4.3 collective-permute-start.11
  117.8 4.2 collective-permute-start.25
  131.0 7.0 collective-permute-start.22
  138.0 3.9 collective-permute-start.27
  155.1 5.0 collective-permute-done.15
  163.8 4.6 copy.126
  170.9 399.6 %while.52 = (s32[]{:T(128)}, f32[3,640,640]{2,1,0:T(8,128)}, f32[128,128]{1,0:T(8,128)S(1)}, f32[128,128]{1,0:T(8,128)S(1)}, f32[128,128]{1,0:T(8,128)S(1)}, /*i...) while((s32[]{:T(128)}, f32[3,640,640]{2,1,0:T(8,128)}, ...), condition=%wide.region_16.20_spmd.clone.clone, body=%wide.region_10.19_spmd.clone.clone.sunk | while | flops 3232875776 | bytes 34477920 | solution.py:181
  175.1 24.4 %while.53 = (s32[]{:T(128)}, f32[2,640,640]{2,1,0:T(8,128)}, s32[8,3]{1,0:T(8,128)S(1)}, f32[8,2,128,128]{3,2,0,1:T(8,128)S(1)}, s32[]{:T(128)}) while((s32[]{:T(128)}, f32[2,640,640]{2,1,0:T(8,128)}, s32[8,3]{1,0:T(8,128)S(1)}, f32[8,2,128,128]{3,2,0,1:T(8,128)S(1)}, s32[]{:T(128)}) %tuple.186), condition=%wide.while_cond.4, body=%wide.while_body.4.sunk | while | flops 2 | bytes 262269 | solution.py:165
  218.6 85.6 %while.54 = (s32[]{:T(128)}, f32[3,640,640]{2,1,0:T(8,128)}, s32[8]{0:T(128)S(1)}, s32[8]{0:T(128)S(1)}, f32[8,3,128,128]{3,2,0,1:T(8,128)S(1)}, /*index=5*/s32[]{:T(128)}, s32[]{:T(128)}, s32[]{:T(128)}) while((s32[]{:T(128)}, f32[3,640,640]{2,1,0:T(8,128)}, s32[8]{0:T(128)S(1)}, s32[8]{0:T(128)S(1)}, f32[8,3,128,128]{3,2,0,1:T(8,128)S(1)}, ...), condition=%wide.region_12.15_spmd, body=%wide.region_11.14_spmd.sunk | while | flops 49160 | bytes 983241 | solution.py:95
  225.3 4.0 dynamic_update_slice.8
  236.0 4.0 dynamic_update_slice.8
  246.7 4.0 dynamic_update_slice.8
  257.4 4.1 dynamic_update_slice.8
  268.1 4.0 dynamic_update_slice.8
  278.8 4.0 dynamic_update_slice.8
  289.5 4.0 dynamic_update_slice.8
  300.2 4.0 dynamic_update_slice.8
  308.5 24.4 %while.53 = (s32[]{:T(128)}, f32[2,640,640]{2,1,0:T(8,128)}, s32[8,3]{1,0:T(8,128)S(1)}, f32[8,2,128,128]{3,2,0,1:T(8,128)S(1)}, s32[]{:T(128)}) while((s32[]{:T(128)}, f32[2,640,640]{2,1,0:T(8,128)}, s32[8,3]{1,0:T(8,128)S(1)}, f32[8,2,128,128]{3,2,0,1:T(8,128)S(1)}, s32[]{:T(128)}) %tuple.186), condition=%wide.while_cond.4, body=%wide.while_body.4.sunk | while | flops 2 | bytes 262269 | solution.py:165
  352.0 85.3 %while.54 = (s32[]{:T(128)}, f32[3,640,640]{2,1,0:T(8,128)}, s32[8]{0:T(128)S(1)}, s32[8]{0:T(128)S(1)}, f32[8,3,128,128]{3,2,0,1:T(8,128)S(1)}, /*index=5*/s32[]{:T(128)}, s32[]{:T(128)}, s32[]{:T(128)}) while((s32[]{:T(128)}, f32[3,640,640]{2,1,0:T(8,128)}, s32[8]{0:T(128)S(1)}, s32[8]{0:T(128)S(1)}, f32[8,3,128,128]{3,2,0,1:T(8,128)S(1)}, ...), condition=%wide.region_12.15_spmd, body=%wide.region_11.14_spmd.sunk | while | flops 49160 | bytes 983241 | solution.py:95
  358.7 4.1 dynamic_update_slice.8
  369.4 3.9 dynamic_update_slice.8
  390.4 4.1 dynamic_update_slice.8
  401.2 4.1 dynamic_update_slice.8
  411.9 4.0 dynamic_update_slice.8
  422.6 4.0 dynamic_update_slice.8
  433.3 4.0 dynamic_update_slice.8
  441.5 24.4 %while.53 = (s32[]{:T(128)}, f32[2,640,640]{2,1,0:T(8,128)}, s32[8,3]{1,0:T(8,128)S(1)}, f32[8,2,128,128]{3,2,0,1:T(8,128)S(1)}, s32[]{:T(128)}) while((s32[]{:T(128)}, f32[2,640,640]{2,1,0:T(8,128)}, s32[8,3]{1,0:T(8,128)S(1)}, f32[8,2,128,128]{3,2,0,1:T(8,128)S(1)}, s32[]{:T(128)}) %tuple.186), condition=%wide.while_cond.4, body=%wide.while_body.4.sunk | while | flops 2 | bytes 262269 | solution.py:165
  485.0 85.4 %while.54 = (s32[]{:T(128)}, f32[3,640,640]{2,1,0:T(8,128)}, s32[8]{0:T(128)S(1)}, s32[8]{0:T(128)S(1)}, f32[8,3,128,128]{3,2,0,1:T(8,128)S(1)}, /*index=5*/s32[]{:T(128)}, s32[]{:T(128)}, s32[]{:T(128)}) while((s32[]{:T(128)}, f32[3,640,640]{2,1,0:T(8,128)}, s32[8]{0:T(128)S(1)}, s32[8]{0:T(128)S(1)}, f32[8,3,128,128]{3,2,0,1:T(8,128)S(1)}, ...), condition=%wide.region_12.15_spmd, body=%wide.region_11.14_spmd.sunk | while | flops 49160 | bytes 983241 | solution.py:95
  491.7 4.1 dynamic_update_slice.8
  502.4 4.1 dynamic_update_slice.8
  534.3 4.1 dynamic_update_slice.8
  545.0 4.1 dynamic_update_slice.8
  555.7 4.1 dynamic_update_slice.8
  566.4 4.0 dynamic_update_slice.8
  571.6 4.3 collective-permute-start.28
  575.9 5.8 collective-permute-done.28
  586.5 135.1 %collective-permute-done.29 = f32[3,64,640]{2,1,0:T(8,128)S(1)} collective-permute-done((f32[3,64,640]{2,1,0:T(8,128)S(1)}, f32[3,64,640]{2,1,0:T(8,128)S(1)}, u32[]{:S(2)}, u32[]{:S(2)}) %collective-permute-start.29) | collective-permute-done | bytes 491552 | tf_op jit(solution)/shard_map/ppermute | solution.py:31
  725.4 13.1 %collective-permute-start.30 = (f32[3,640,64]{1,2,0:T(8,128)S(1)}, f32[3,640,64]{1,2,0:T(8,128)S(1)}, u32[]{:S(2)}, u32[]{:S(2)}) collective-permute-start(f32[3,640,64]{1,2,0:T(8,128)S(1)} %copy.127), channel_id=1, source_target_pairs={{0,1},{1,2},{2,3},{3,4},{4,5},{5,6},{6,7},{7,8},{8,9},{9,10},{10,1... | collective-permute-start | bytes 1474568 | tf_op jit(solution)/shard_map/ppermute | solution.py:31
  738.5 5.7 collective-permute-done.30
  746.1 9.2 scatter-add.16
  758.1 259.3 %all-reduce.3.cloned.1.call-done = (f32[1,128,128]{2,1,0:T(8,128)}, f32[1,128,128]{2,1,0:T(8,128)}, f32[128,128]{1,0:T(8,128)}) async-done(((f32[1,128,128]{2,1,0:T(8,128)}, f32[1,128,128]{2,1,0:T(8,128)}, f32[128,128]{1,0:T(8,128)}), (f32[1,128,128]{2,1,0:T(8,128)}, f32[1,128,128]{2,1,0:T(8,128)}, f32[128,128]{1,0:T(8,128)})) %all-reduce.3.cloned.1.call-update) | async-done | bytes 196624 | tf_op jit(solution)/shard_map/psum | solution.py:208
  1022.8 7.0 scatter-add.19
  (445 shorter events, 343.2 us)
Async XLA Ops:
  7.2 35.9 %copy-start.2 = (f32[1,1,32,128,128]{4,3,2,1,0:T(8,128)S(1)}, f32[1,1,32,128,128]{4,3,2,1,0:T(8,128)}, u32[]{:S(2)}) copy-start(f32[1,1,32,128,128]{4,3,2,1,0:T(8,128)} %param.24) | copy-start | bytes 6291460
  7.2 1010.2 %all-reduce.3.cloned.1.call-start = ((), (), s32[]{:S(2)}) async-start(), calls=%async_computation | async-start | bytes 393216 | tf_op jit(solution)/shard_map/psum | solution.py:208
  13.9 65.7 %collective-permute-start = (s32[2,3]{1,0:T(2,128)S(1)}, s32[2,3]{1,0:T(2,128)}, u32[]{:S(2)}, u32[]{:S(2)}) collective-permute-start(s32[2,3]{1,0:T(2,128)S(1)} %select_select_fusion.7), channel_id=1, source_target_pairs={{1,0},{2,1},{3,2},{4,3},{5,4},{6,5},{7,6},{8,7},{9,8},{10,9},{11,1... | collective-permute-start | bytes 80 | tf_op jit(solution)/shard_map/ppermute | solution.py:31
  16.5 48.0 %collective-permute-start.2 = (s32[2,3]{1,0:T(2,128)S(1)}, s32[2,3]{1,0:T(2,128)S(1)}, u32[]{:S(2)}, u32[]{:S(2)}) collective-permute-start(s32[2,3]{1,0:T(2,128)S(1)} %select_select_fusion.6), channel_id=1, source_target_pairs={{16,0},{32,16},{48,32},{64,48},{80,64},{96,80},{112,96},{17,1},{33... | collective-permute-start | bytes 80 | tf_op jit(solution)/shard_map/ppermute | solution.py:31
  24.3 61.1 %collective-permute-start.3 = (s32[2,3]{1,0:T(2,128)S(1)}, s32[2,3]{1,0:T(2,128)}, u32[]{:S(2)}, u32[]{:S(2)}) collective-permute-start(s32[2,3]{1,0:T(2,128)S(1)} %select_select_fusion.5), channel_id=1, source_target_pairs={{0,1},{1,2},{2,3},{3,4},{4,5},{5,6},{6,7},{7,8},{8,9},{9,10},{10,1... | collective-permute-start | bytes 80 | tf_op jit(solution)/shard_map/ppermute | solution.py:31
  30.4 35.4 %collective-permute-start.5 = (s32[2,3]{1,0:T(2,128)S(1)}, s32[2,3]{1,0:T(2,128)S(1)}, u32[]{:S(2)}, u32[]{:S(2)}) collective-permute-start(s32[2,3]{1,0:T(2,128)S(1)} %select_select_fusion.4), channel_id=1, source_target_pairs={{1,0},{2,1},{3,2},{4,3},{5,4},{6,5},{7,6},{8,7},{9,8},{10,9},{11,1... | collective-permute-start | bytes 80 | tf_op jit(solution)/shard_map/ppermute | solution.py:31
  36.8 33.0 %collective-permute-start.6 = (s32[2,3]{1,0:T(2,128)}, s32[2,3]{1,0:T(2,128)S(1)}, u32[]{:S(2)}, u32[]{:S(2)}) collective-permute-start(s32[2,3]{1,0:T(2,128)} %select_select_fusion.3), channel_id=1, source_target_pairs={{0,1},{1,2},{2,3},{3,4},{4,5},{5,6},{6,7},{7,8},{8,9},{9,10},{10,1... | collective-permute-start | bytes 80 | tf_op jit(solution)/shard_map/ppermute | solution.py:31
  50.3 6.3 copy-start.1
  60.2 3.9 copy-start.6
  60.2 4.1 copy-start.7
  64.4 32.5 %collective-permute-start.7 = (s32[2,3]{1,0:T(2,128)S(1)}, s32[2,3]{1,0:T(2,128)S(1)}, u32[]{:S(2)}, u32[]{:S(2)}) collective-permute-start(s32[2,3]{1,0:T(2,128)S(1)} %select_select_fusion.2), channel_id=1, source_target_pairs={{1,0},{2,1},{3,2},{4,3},{5,4},{6,5},{7,6},{8,7},{9,8},{10,9},{11,1... | collective-permute-start | bytes 80 | tf_op jit(solution)/shard_map/ppermute | solution.py:31
  65.8 8.4 collective-permute-start.9
  69.9 29.0 %collective-permute-start.10 = (s32[2,3]{1,0:T(2,128)S(1)}, s32[2,3]{1,0:T(2,128)S(1)}, u32[]{:S(2)}, u32[]{:S(2)}) collective-permute-start(s32[2,3]{1,0:T(2,128)S(1)} %select_select_fusion), channel_id=1, source_target_pairs={{0,1},{1,2},{2,3},{3,4},{4,5},{5,6},{6,7},{7,8},{8,9},{9,10},{10,1... | collective-permute-start | bytes 80 | tf_op jit(solution)/shard_map/ppermute | solution.py:31
  74.2 56.7 %collective-permute-start.26 = (f32[2,128,128]{2,1,0:T(8,128)}, f32[2,128,128]{2,1,0:T(8,128)}, u32[]{:S(2)}, u32[]{:S(2)}) collective-permute-start(f32[2,128,128]{2,1,0:T(8,128)} %broadcast_select_fusion.1), channel_id=1, source_target_pairs={{0,1},{1,2},{2,3},{3,4},{4,5},{5,6},{6,7},{7,8},{8,9},{9,10},{10,1... | collective-permute-start | bytes 393224 | tf_op jit(solution)/shard_map/ppermute | solution.py:31
  79.6 45.5 %collective-permute-start.19 = (f32[2,128,128]{2,1,0:T(8,128)}, f32[2,128,128]{2,1,0:T(8,128)}, u32[]{:S(2)}, u32[]{:S(2)}) collective-permute-start(f32[2,128,128]{2,1,0:T(8,128)} %broadcast_select_fusion.6), channel_id=1, source_target_pairs={{0,1},{1,2},{2,3},{3,4},{4,5},{5,6},{6,7},{7,8},{8,9},{9,10},{10,1... | collective-permute-start | bytes 393224 | tf_op jit(solution)/shard_map/ppermute | solution.py:31
  85.3 5.1 collective-permute-start.1
  90.4 5.1 collective-permute-start.4
  95.5 16.9 %collective-permute-start.16 = (f32[2,128,128]{2,1,0:T(8,128)}, f32[2,128,128]{2,1,0:T(8,128)}, u32[]{:S(2)}, u32[]{:S(2)}) collective-permute-start(f32[2,128,128]{2,1,0:T(8,128)} %broadcast_select_fusion.8), channel_id=1, source_target_pairs={{1,0},{2,1},{3,2},{4,3},{5,4},{6,5},{7,6},{8,7},{9,8},{10,9},{11,1... | collective-permute-start | bytes 393224 | tf_op jit(solution)/shard_map/ppermute | solution.py:31
  96.9 20.9 %collective-permute-start.12 = (f32[2,64,512]{1,2,0:T(8,128)}, f32[2,64,512]{1,2,0:T(8,128)S(1)}, u32[]{:S(2)}, u32[]{:S(2)}) collective-permute-start(f32[2,64,512]{1,2,0:T(8,128)} %get-tuple-element.723), channel_id=1, source_target_pairs={{0,16},{16,32},{32,48},{48,64},{64,80},{80,96},{96,112},{1,17},{17... | collective-permute-start | bytes 786440 | tf_op jit(solution)/shard_map/ppermute | solution.py:22
  98.9 6.4 collective-permute-start.8
  105.3 5.0 collective-permute-start.11
  110.3 11.7 %collective-permute-start.13 = (f32[2,64,512]{1,2,0:T(8,128)}, f32[2,64,512]{1,2,0:T(8,128)}, u32[]{:S(2)}, u32[]{:S(2)}) collective-permute-start(f32[2,64,512]{1,2,0:T(8,128)} %get-tuple-element.724), channel_id=1, source_target_pairs={{16,0},{32,16},{48,32},{64,48},{80,64},{96,80},{112,96},{17,1},{33... | collective-permute-start | bytes 786440 | tf_op jit(solution)/shard_map/ppermute | solution.py:23
  112.4 14.0 %collective-permute-start.17 = (f32[2,128,128]{2,1,0:T(8,128)}, f32[2,128,128]{2,1,0:T(8,128)S(1)}, u32[]{:S(2)}, u32[]{:S(2)}) collective-permute-start(f32[2,128,128]{2,1,0:T(8,128)} %collective-permute-done.16), channel_id=1, source_target_pairs={{16,0},{32,16},{48,32},{64,48},{80,64},{96,80},{112,96},{17,1},{33... | collective-permute-start | bytes 393224 | tf_op jit(solution)/shard_map/ppermute | solution.py:31
  117.8 33.8 %collective-permute-start.25 = (f32[2,128,128]{2,1,0:T(8,128)S(1)}, f32[2,128,128]{2,1,0:T(8,128)S(1)}, u32[]{:S(2)}, u32[]{:S(2)}) collective-permute-start(f32[2,128,128]{2,1,0:T(8,128)S(1)} %broadcast_select_fusion.2), channel_id=1, source_target_pairs={{0,16},{16,32},{32,48},{48,64},{64,80},{80,96},{96,112},{1,17},{17... | collective-permute-start | bytes 393224 | tf_op jit(solution)/shard_map/ppermute | solution.py:31
  122.0 7.0 collective-permute-start.18
  125.1 12.9 %collective-permute-start.23 = (f32[2,128,128]{2,1,0:T(8,128)S(1)}, f32[2,128,128]{2,1,0:T(8,128)S(1)}, u32[]{:S(2)}, u32[]{:S(2)}) collective-permute-start(f32[2,128,128]{2,1,0:T(8,128)S(1)} %broadcast_select_fusion.3), channel_id=1, source_target_pairs={{1,0},{2,1},{3,2},{4,3},{5,4},{6,5},{7,6},{8,7},{9,8},{10,9},{11,1... | collective-permute-start | bytes 393224 | tf_op jit(solution)/shard_map/ppermute | solution.py:31
  126.4 15.5 %collective-permute-start.20 = (f32[2,128,128]{2,1,0:T(8,128)}, f32[2,128,128]{2,1,0:T(8,128)S(1)}, u32[]{:S(2)}, u32[]{:S(2)}) collective-permute-start(f32[2,128,128]{2,1,0:T(8,128)} %collective-permute-done.19), channel_id=1, source_target_pairs={{16,0},{32,16},{48,32},{64,48},{80,64},{96,80},{112,96},{17,1},{33... | collective-permute-start | bytes 393224 | tf_op jit(solution)/shard_map/ppermute | solution.py:31
  129.0 15.7 %collective-permute-start.21 = (f32[2,128,128]{2,1,0:T(8,128)}, f32[2,128,128]{2,1,0:T(8,128)S(1)}, u32[]{:S(2)}, u32[]{:S(2)}) collective-permute-start(f32[2,128,128]{2,1,0:T(8,128)} %broadcast_select_fusion.5), channel_id=1, source_target_pairs={{1,0},{2,1},{3,2},{4,3},{5,4},{6,5},{7,6},{8,7},{9,8},{10,9},{11,1... | collective-permute-start | bytes 393224 | tf_op jit(solution)/shard_map/ppermute | solution.py:31
  131.0 18.1 %collective-permute-start.22 = (f32[2,128,128]{2,1,0:T(8,128)}, f32[2,128,128]{2,1,0:T(8,128)S(1)}, u32[]{:S(2)}, u32[]{:S(2)}) collective-permute-start(f32[2,128,128]{2,1,0:T(8,128)} %broadcast_select_fusion.4), channel_id=1, source_target_pairs={{0,1},{1,2},{2,3},{3,4},{4,5},{5,6},{6,7},{7,8},{8,9},{9,10},{10,1... | collective-permute-start | bytes 393224 | tf_op jit(solution)/shard_map/ppermute | solution.py:31
  138.0 14.3 %collective-permute-start.27 = (f32[2,128,128]{2,1,0:T(8,128)}, f32[2,128,128]{2,1,0:T(8,128)S(1)}, u32[]{:S(2)}, u32[]{:S(2)}) collective-permute-start(f32[2,128,128]{2,1,0:T(8,128)} %collective-permute-done.26), channel_id=1, source_target_pairs={{0,16},{16,32},{32,48},{48,64},{64,80},{80,96},{96,112},{1,17},{17... | collective-permute-start | bytes 393224 | tf_op jit(solution)/shard_map/ppermute | solution.py:31
  141.9 9.1 collective-permute-start.24
  144.7 10.4 collective-permute-start.14
  149.0 11.1 %collective-permute-start.15 = (f32[2,640,64]{1,2,0:T(8,128)S(1)}, f32[2,640,64]{1,2,0:T(8,128)S(1)}, u32[]{:S(2)}, u32[]{:S(2)}) collective-permute-start(f32[2,640,64]{1,2,0:T(8,128)S(1)} %get-tuple-element.722), channel_id=1, source_target_pairs={{1,0},{2,1},{3,2},{4,3},{5,4},{6,5},{7,6},{8,7},{9,8},{10,9},{11,1... | collective-permute-start | bytes 983048 | tf_op jit(solution)/shard_map/ppermute | solution.py:23
  570.5 154.6 %copy-start.3 = (f32[128,128]{1,0:T(8,128)}, f32[128,128]{1,0:T(8,128)S(1)}, u32[]{:S(2)}) copy-start(f32[128,128]{1,0:T(8,128)S(1)} %get-tuple-element.452) | copy-start | bytes 196612
  570.5 154.6 %copy-start.4 = (f32[128,128]{1,0:T(8,128)}, f32[128,128]{1,0:T(8,128)S(1)}, u32[]{:S(2)}) copy-start(f32[128,128]{1,0:T(8,128)S(1)} %get-tuple-element.451) | copy-start | bytes 196612
  570.5 154.6 %copy-start.5 = (f32[128,128]{1,0:T(8,128)}, f32[128,128]{1,0:T(8,128)S(1)}, u32[]{:S(2)}) copy-start(f32[128,128]{1,0:T(8,128)S(1)} %get-tuple-element.450) | copy-start | bytes 196612
  571.6 10.0 collective-permute-start.28
  584.6 137.0 %collective-permute-start.29 = (f32[3,64,640]{2,1,0:T(8,128)S(1)}, f32[3,64,640]{2,1,0:T(8,128)S(1)}, u32[]{:S(2)}, u32[]{:S(2)}) collective-permute-start(f32[3,64,640]{2,1,0:T(8,128)S(1)} %slice.318), channel_id=1, source_target_pairs={{16,0},{32,16},{48,32},{64,48},{80,64},{96,80},{112,96},{17,1},{33... | collective-permute-start | bytes 1474568 | tf_op jit(solution)/shard_map/ppermute | solution.py:31
  725.4 18.8 %collective-permute-start.30 = (f32[3,640,64]{1,2,0:T(8,128)S(1)}, f32[3,640,64]{1,2,0:T(8,128)S(1)}, u32[]{:S(2)}, u32[]{:S(2)}) collective-permute-start(f32[3,640,64]{1,2,0:T(8,128)S(1)} %copy.127), channel_id=1, source_target_pairs={{0,1},{1,2},{2,3},{3,4},{4,5},{5,6},{6,7},{7,8},{8,9},{9,10},{10,1... | collective-permute-start | bytes 1474568 | tf_op jit(solution)/shard_map/ppermute | solution.py:31
  756.8 263.0 %collective-permute-start.31 = (f32[3,640,64]{1,2,0:T(8,128)S(1)}, f32[3,640,64]{1,2,0:T(8,128)S(1)}, u32[]{:S(2)}, u32[]{:S(2)}) collective-permute-start(f32[3,640,64]{1,2,0:T(8,128)S(1)} %copy.129), channel_id=1, source_target_pairs={{1,0},{2,1},{3,2},{4,3},{5,4},{6,5},{7,6},{8,7},{9,8},{10,9},{11,1... | collective-permute-start | bytes 1474568 | tf_op jit(solution)/shard_map/ppermute | solution.py:31
  1021.1 10.4 copy-start
Sparse Core Ops, SparseCore 0:
  738.6 278.7 all-reduce.2
where the time goes:
time: 1050 us; the launch traced here: 1040 us
  waiting for transfers between devices  423 us (40%)
  local copies, waits for them, and re-layouts  269 us (26%)
  starting transfers between devices  103 us (10%)
  loops' own time  101 us (10%)
  other arithmetic  73.1 us (7%)
  matrix products  56.2 us (5%)
  between operations  16.2 us (2%)
    psum x1, waiting for transfers between devices, shards(): summed = lax.psum((grad_real, grad_imag, weight), ('ty', 'tx'))  259 us
    ppermute x28, waiting for transfers between devices, from_behind(): return lax.ppermute(block, axis, route)  156 us
    another operation x3, loops' own time, add_patches(): return lax.fori_loop(0, spread.shape[0], add_one, accumulated)  100 us
    dynamic_update_slice x24, local copies, waits for them, and re-layouts, add_one(): lax.dynamic_update_slice(current, window + spread[patch_id], (zero_index,...  96.4 us
    ppermute x28, starting transfers between devices, from_behind(): return lax.ppermute(block, axis, route)  94.2 us
    gather x72, local copies, waits for them, and re-layouts  72.6 us
    add x24, other arithmetic, add_one(): window + spread[patch_id]  27.6 us
  transfers between devices with their start and end apart: 33, of which 10 were waited for; matrix products, arithmetic and copies ran while one was open for 6% of the time, Pallas kernels for 0%

commit v1 on v0

--- a/solution.py
+++ b/solution.py
@@ -205,7 +205,9 @@
             accumulated = accumulated.at[:, :, tile_cols : tile_cols + rim_width].add(arrived)
     interior = accumulated[:, rim_width : rim_width + tile_rows, rim_width : rim_width + tile_cols]
     new_object = object_field - interior[:2] / (interior[2] + floor_level)
-    summed = lax.psum((grad_real, grad_imag, weight), ("ty", "tx"))
+    summed = (grad_real, grad_imag, weight)
+    for j0 in ("ty", "tx"):
+        summed = lax.psum(summed, j0)
     new_probe = probe_field - jnp.stack([summed[0], summed[1]]) / (summed[2] + tiny_level)
     return (new_object, new_probe)
 

time: 1050 us -> 1060 us (level)
    psum x1 -> x2, waiting for transfers between devices: 259 us -> 271 us  [shards(): summed = lax.psum(summed, j0)]
  transfers between devices with their start and end apart: 33 -> 34, of which waited for: 10 -> 10; matrix products, arithmetic and copies ran while one was open for 6% -> 6% of each run, Pallas kernels for 0% -> 0%
where the time goes in v1:
time: 1060 us; the launch traced here: 1050 us
  waiting for transfers between devices  429 us (40%)
  local copies, waits for them, and re-layouts  269 us (25%)
  starting transfers between devices  103 us (10%)
  loops' own time  101 us (10%)
  other arithmetic  73.1 us (7%)
  matrix products  56.2 us (5%)
  between operations  16.2 us (2%)
    psum x2, waiting for transfers between devices, shards(): summed = lax.psum(summed, j0)  271 us
    ppermute x28, waiting for transfers between devices, from_behind(): return lax.ppermute(block, axis, route)  151 us
    another operation x3, loops' own time, add_patches(): return lax.fori_loop(0, spread.shape[0], add_one, accumulated)  100 us
    dynamic_update_slice x24, local copies, waits for them, and re-layouts, add_one(): lax.dynamic_update_slice(current, window + spread[patch_id], (zero_index,...  96.4 us
    ppermute x28, starting transfers between devices, from_behind(): return lax.ppermute(block, axis, route)  94.2 us
    gather x72, local copies, waits for them, and re-layouts  72.6 us
    add x24, other arithmetic, add_one(): window + spread[patch_id]  27.6 us
  transfers between devices with their start and end apart: 34, of which 10 were waited for; matrix products, arithmetic and copies ran while one was open for 6% of the time, Pallas kernels for 0%

profile of v1, /device:TPU:1, one launch (start us, length us, event | category | flops | bytes accessed | tf_op | source)
XLA Modules:
  0.0 1048.2 jit_solution(14792590855650351858)
XLA Ops:
  24.3 4.9 collective-permute-start.3
  36.8 4.0 collective-permute-start.6
  65.8 3.9 collective-permute-start.9
  69.9 4.3 collective-permute-start.10
  74.2 5.3 collective-permute-start.26
  79.6 5.7 collective-permute-start.19
  105.3 4.3 collective-permute-start.11
  117.8 4.2 collective-permute-start.25
  131.0 7.0 collective-permute-start.22
  138.0 3.9 collective-permute-start.27
  155.1 5.0 collective-permute-done.15
  163.8 4.6 copy.126
  170.9 399.6 %while.52 = (s32[]{:T(128)}, f32[3,640,640]{2,1,0:T(8,128)}, f32[128,128]{1,0:T(8,128)S(1)}, f32[128,128]{1,0:T(8,128)S(1)}, f32[128,128]{1,0:T(8,128)S(1)}, /*i...) while((s32[]{:T(128)}, f32[3,640,640]{2,1,0:T(8,128)}, ...), condition=%wide.region_16.20_spmd.clone.clone, body=%wide.region_10.19_spmd.clone.clone.sunk | while | flops 3232875776 | bytes 34477920 | solution.py:181
  175.1 24.4 %while.53 = (s32[]{:T(128)}, f32[2,640,640]{2,1,0:T(8,128)}, s32[8,3]{1,0:T(8,128)S(1)}, f32[8,2,128,128]{3,2,0,1:T(8,128)S(1)}, s32[]{:T(128)}) while((s32[]{:T(128)}, f32[2,640,640]{2,1,0:T(8,128)}, s32[8,3]{1,0:T(8,128)S(1)}, f32[8,2,128,128]{3,2,0,1:T(8,128)S(1)}, s32[]{:T(128)}) %tuple.186), condition=%wide.while_cond.4, body=%wide.while_body.4.sunk | while | flops 2 | bytes 262269 | solution.py:165
  218.6 85.6 %while.54 = (s32[]{:T(128)}, f32[3,640,640]{2,1,0:T(8,128)}, s32[8]{0:T(128)S(1)}, s32[8]{0:T(128)S(1)}, f32[8,3,128,128]{3,2,0,1:T(8,128)S(1)}, /*index=5*/s32[]{:T(128)}, s32[]{:T(128)}, s32[]{:T(128)}) while((s32[]{:T(128)}, f32[3,640,640]{2,1,0:T(8,128)}, s32[8]{0:T(128)S(1)}, s32[8]{0:T(128)S(1)}, f32[8,3,128,128]{3,2,0,1:T(8,128)S(1)}, ...), condition=%wide.region_12.15_spmd, body=%wide.region_11.14_spmd.sunk | while | flops 49160 | bytes 983241 | solution.py:95
  225.3 4.0 dynamic_update_slice.8
  236.0 4.0 dynamic_update_slice.8
  246.7 4.0 dynamic_update_slice.8
  257.4 4.1 dynamic_update_slice.8
  268.1 4.0 dynamic_update_slice.8
  278.8 4.0 dynamic_update_slice.8
  289.5 4.0 dynamic_update_slice.8
  300.2 4.0 dynamic_update_slice.8
  308.5 24.4 %while.53 = (s32[]{:T(128)}, f32[2,640,640]{2,1,0:T(8,128)}, s32[8,3]{1,0:T(8,128)S(1)}, f32[8,2,128,128]{3,2,0,1:T(8,128)S(1)}, s32[]{:T(128)}) while((s32[]{:T(128)}, f32[2,640,640]{2,1,0:T(8,128)}, s32[8,3]{1,0:T(8,128)S(1)}, f32[8,2,128,128]{3,2,0,1:T(8,128)S(1)}, s32[]{:T(128)}) %tuple.186), condition=%wide.while_cond.4, body=%wide.while_body.4.sunk | while | flops 2 | bytes 262269 | solution.py:165
  352.0 85.3 %while.54 = (s32[]{:T(128)}, f32[3,640,640]{2,1,0:T(8,128)}, s32[8]{0:T(128)S(1)}, s32[8]{0:T(128)S(1)}, f32[8,3,128,128]{3,2,0,1:T(8,128)S(1)}, /*index=5*/s32[]{:T(128)}, s32[]{:T(128)}, s32[]{:T(128)}) while((s32[]{:T(128)}, f32[3,640,640]{2,1,0:T(8,128)}, s32[8]{0:T(128)S(1)}, s32[8]{0:T(128)S(1)}, f32[8,3,128,128]{3,2,0,1:T(8,128)S(1)}, ...), condition=%wide.region_12.15_spmd, body=%wide.region_11.14_spmd.sunk | while | flops 49160 | bytes 983241 | solution.py:95
  358.7 4.1 dynamic_update_slice.8
  369.4 3.9 dynamic_update_slice.8
  390.4 4.1 dynamic_update_slice.8
  401.2 4.1 dynamic_update_slice.8
  411.9 4.0 dynamic_update_slice.8
  422.6 4.0 dynamic_update_slice.8
  433.3 4.0 dynamic_update_slice.8
  441.5 24.4 %while.53 = (s32[]{:T(128)}, f32[2,640,640]{2,1,0:T(8,128)}, s32[8,3]{1,0:T(8,128)S(1)}, f32[8,2,128,128]{3,2,0,1:T(8,128)S(1)}, s32[]{:T(128)}) while((s32[]{:T(128)}, f32[2,640,640]{2,1,0:T(8,128)}, s32[8,3]{1,0:T(8,128)S(1)}, f32[8,2,128,128]{3,2,0,1:T(8,128)S(1)}, s32[]{:T(128)}) %tuple.186), condition=%wide.while_cond.4, body=%wide.while_body.4.sunk | while | flops 2 | bytes 262269 | solution.py:165
  485.0 85.4 %while.54 = (s32[]{:T(128)}, f32[3,640,640]{2,1,0:T(8,128)}, s32[8]{0:T(128)S(1)}, s32[8]{0:T(128)S(1)}, f32[8,3,128,128]{3,2,0,1:T(8,128)S(1)}, /*index=5*/s32[]{:T(128)}, s32[]{:T(128)}, s32[]{:T(128)}) while((s32[]{:T(128)}, f32[3,640,640]{2,1,0:T(8,128)}, s32[8]{0:T(128)S(1)}, s32[8]{0:T(128)S(1)}, f32[8,3,128,128]{3,2,0,1:T(8,128)S(1)}, ...), condition=%wide.region_12.15_spmd, body=%wide.region_11.14_spmd.sunk | while | flops 49160 | bytes 983241 | solution.py:95
  491.7 4.1 dynamic_update_slice.8
  502.4 4.1 dynamic_update_slice.8
  534.3 4.1 dynamic_update_slice.8
  545.0 4.1 dynamic_update_slice.8
  555.7 4.1 dynamic_update_slice.8
  566.4 4.0 dynamic_update_slice.8
  571.6 4.3 collective-permute-start.28
  575.9 5.8 collective-permute-done.28
  586.5 135.1 %collective-permute-done.29 = f32[3,64,640]{2,1,0:T(8,128)S(1)} collective-permute-done((f32[3,64,640]{2,1,0:T(8,128)S(1)}, f32[3,64,640]{2,1,0:T(8,128)S(1)}, u32[]{:S(2)}, u32[]{:S(2)}) %collective-permute-start.29) | collective-permute-done | bytes 491552 | tf_op jit(solution)/shard_map/ppermute | solution.py:31
  725.4 13.1 %collective-permute-start.30 = (f32[3,640,64]{1,2,0:T(8,128)S(1)}, f32[3,640,64]{1,2,0:T(8,128)S(1)}, u32[]{:S(2)}, u32[]{:S(2)}) collective-permute-start(f32[3,640,64]{1,2,0:T(8,128)S(1)} %copy.127), channel_id=1, source_target_pairs={{0,1},{1,2},{2,3},{3,4},{4,5},{5,6},{6,7},{7,8},{8,9},{9,10},{10,1... | collective-permute-start | bytes 1474568 | tf_op jit(solution)/shard_map/ppermute | solution.py:31
  738.5 191.2 %all-reduce.7.cloned.1.call-done = (f32[128,128]{1,0:T(8,128)}, f32[128,128]{1,0:T(8,128)}, f32[128,128]{1,0:T(8,128)}) async-done(((f32[128,128]{1,0:T(8,128)}, f32[128,128]{1,0:T(8,128)}, f32[128,128]{1,0:T(8,128)}), (f32[128,128]{1,0:T(8,128)}, f32[128,128]{1,0:T(8,128)}, f32[128,128]{1,0:T(8,128)})) %all-reduce.7.cloned.1.call-update) | async-done | bytes 196624 | tf_op jit(solution)/shard_map/psum | solution.py:210
  931.7 9.2 scatter-add.16
  943.8 79.9 %all-reduce.5.cloned.1.call-done = (f32[1,128,128]{2,1,0:T(8,128)}, f32[1,128,128]{2,1,0:T(8,128)}, f32[128,128]{1,0:T(8,128)}) async-done(((f32[1,128,128]{2,1,0:T(8,128)}, f32[1,128,128]{2,1,0:T(8,128)}, f32[128,128]{1,0:T(8,128)}), (f32[1,128,128]{2,1,0:T(8,128)}, f32[1,128,128]{2,1,0:T(8,128)}, f32[128,128]{1,0:T(8,128)})) %all-reduce.5.cloned.1.call-update) | async-done | bytes 196624 | tf_op jit(solution)/shard_map/psum | solution.py:210
  1029.1 7.0 scatter-add.19
  (448 shorter events, 343.2 us)
Async XLA Ops:
  7.2 35.9 %copy-start.2 = (f32[1,1,32,128,128]{4,3,2,1,0:T(8,128)S(1)}, f32[1,1,32,128,128]{4,3,2,1,0:T(8,128)}, u32[]{:S(2)}) copy-start(f32[1,1,32,128,128]{4,3,2,1,0:T(8,128)} %param.24) | copy-start | bytes 6291460
  7.2 922.6 %all-reduce.7.cloned.1.call-start = ((), (), s32[]{:S(2)}) async-start(), calls=%async_computation.1 | async-start | bytes 393216 | tf_op jit(solution)/shard_map/psum | solution.py:210
  13.9 65.7 %collective-permute-start = (s32[2,3]{1,0:T(2,128)S(1)}, s32[2,3]{1,0:T(2,128)}, u32[]{:S(2)}, u32[]{:S(2)}) collective-permute-start(s32[2,3]{1,0:T(2,128)S(1)} %select_select_fusion.7), channel_id=1, source_target_pairs={{1,0},{2,1},{3,2},{4,3},{5,4},{6,5},{7,6},{8,7},{9,8},{10,9},{11,1... | collective-permute-start | bytes 80 | tf_op jit(solution)/shard_map/ppermute | solution.py:31
  16.5 48.0 %collective-permute-start.2 = (s32[2,3]{1,0:T(2,128)S(1)}, s32[2,3]{1,0:T(2,128)S(1)}, u32[]{:S(2)}, u32[]{:S(2)}) collective-permute-start(s32[2,3]{1,0:T(2,128)S(1)} %select_select_fusion.6), channel_id=1, source_target_pairs={{16,0},{32,16},{48,32},{64,48},{80,64},{96,80},{112,96},{17,1},{33... | collective-permute-start | bytes 80 | tf_op jit(solution)/shard_map/ppermute | solution.py:31
  24.3 61.1 %collective-permute-start.3 = (s32[2,3]{1,0:T(2,128)S(1)}, s32[2,3]{1,0:T(2,128)}, u32[]{:S(2)}, u32[]{:S(2)}) collective-permute-start(s32[2,3]{1,0:T(2,128)S(1)} %select_select_fusion.5), channel_id=1, source_target_pairs={{0,1},{1,2},{2,3},{3,4},{4,5},{5,6},{6,7},{7,8},{8,9},{9,10},{10,1... | collective-permute-start | bytes 80 | tf_op jit(solution)/shard_map/ppermute | solution.py:31
  30.4 35.4 %collective-permute-start.5 = (s32[2,3]{1,0:T(2,128)S(1)}, s32[2,3]{1,0:T(2,128)S(1)}, u32[]{:S(2)}, u32[]{:S(2)}) collective-permute-start(s32[2,3]{1,0:T(2,128)S(1)} %select_select_fusion.4), channel_id=1, source_target_pairs={{1,0},{2,1},{3,2},{4,3},{5,4},{6,5},{7,6},{8,7},{9,8},{10,9},{11,1... | collective-permute-start | bytes 80 | tf_op jit(solution)/shard_map/ppermute | solution.py:31
  36.8 33.0 %collective-permute-start.6 = (s32[2,3]{1,0:T(2,128)}, s32[2,3]{1,0:T(2,128)S(1)}, u32[]{:S(2)}, u32[]{:S(2)}) collective-permute-start(s32[2,3]{1,0:T(2,128)} %select_select_fusion.3), channel_id=1, source_target_pairs={{0,1},{1,2},{2,3},{3,4},{4,5},{5,6},{6,7},{7,8},{8,9},{9,10},{10,1... | collective-permute-start | bytes 80 | tf_op jit(solution)/shard_map/ppermute | solution.py:31
  50.3 6.3 copy-start.1
  60.2 3.9 copy-start.6
  60.2 4.1 copy-start.7
  64.4 32.5 %collective-permute-start.7 = (s32[2,3]{1,0:T(2,128)S(1)}, s32[2,3]{1,0:T(2,128)S(1)}, u32[]{:S(2)}, u32[]{:S(2)}) collective-permute-start(s32[2,3]{1,0:T(2,128)S(1)} %select_select_fusion.2), channel_id=1, source_target_pairs={{1,0},{2,1},{3,2},{4,3},{5,4},{6,5},{7,6},{8,7},{9,8},{10,9},{11,1... | collective-permute-start | bytes 80 | tf_op jit(solution)/shard_map/ppermute | solution.py:31
  65.8 8.4 collective-permute-start.9
  69.9 29.0 %collective-permute-start.10 = (s32[2,3]{1,0:T(2,128)S(1)}, s32[2,3]{1,0:T(2,128)S(1)}, u32[]{:S(2)}, u32[]{:S(2)}) collective-permute-start(s32[2,3]{1,0:T(2,128)S(1)} %select_select_fusion), channel_id=1, source_target_pairs={{0,1},{1,2},{2,3},{3,4},{4,5},{5,6},{6,7},{7,8},{8,9},{9,10},{10,1... | collective-permute-start | bytes 80 | tf_op jit(solution)/shard_map/ppermute | solution.py:31
  74.2 56.7 %collective-permute-start.26 = (f32[2,128,128]{2,1,0:T(8,128)}, f32[2,128,128]{2,1,0:T(8,128)}, u32[]{:S(2)}, u32[]{:S(2)}) collective-permute-start(f32[2,128,128]{2,1,0:T(8,128)} %broadcast_select_fusion.1), channel_id=1, source_target_pairs={{0,1},{1,2},{2,3},{3,4},{4,5},{5,6},{6,7},{7,8},{8,9},{9,10},{10,1... | collective-permute-start | bytes 393224 | tf_op jit(solution)/shard_map/ppermute | solution.py:31
  79.6 45.5 %collective-permute-start.19 = (f32[2,128,128]{2,1,0:T(8,128)}, f32[2,128,128]{2,1,0:T(8,128)}, u32[]{:S(2)}, u32[]{:S(2)}) collective-permute-start(f32[2,128,128]{2,1,0:T(8,128)} %broadcast_select_fusion.6), channel_id=1, source_target_pairs={{0,1},{1,2},{2,3},{3,4},{4,5},{5,6},{6,7},{7,8},{8,9},{9,10},{10,1... | collective-permute-start | bytes 393224 | tf_op jit(solution)/shard_map/ppermute | solution.py:31
  85.3 5.1 collective-permute-start.1
  90.4 5.1 collective-permute-start.4
  95.5 16.9 %collective-permute-start.16 = (f32[2,128,128]{2,1,0:T(8,128)}, f32[2,128,128]{2,1,0:T(8,128)}, u32[]{:S(2)}, u32[]{:S(2)}) collective-permute-start(f32[2,128,128]{2,1,0:T(8,128)} %broadcast_select_fusion.8), channel_id=1, source_target_pairs={{1,0},{2,1},{3,2},{4,3},{5,4},{6,5},{7,6},{8,7},{9,8},{10,9},{11,1... | collective-permute-start | bytes 393224 | tf_op jit(solution)/shard_map/ppermute | solution.py:31
  96.9 20.9 %collective-permute-start.12 = (f32[2,64,512]{1,2,0:T(8,128)}, f32[2,64,512]{1,2,0:T(8,128)S(1)}, u32[]{:S(2)}, u32[]{:S(2)}) collective-permute-start(f32[2,64,512]{1,2,0:T(8,128)} %get-tuple-element.726), channel_id=1, source_target_pairs={{0,16},{16,32},{32,48},{48,64},{64,80},{80,96},{96,112},{1,17},{17... | collective-permute-start | bytes 786440 | tf_op jit(solution)/shard_map/ppermute | solution.py:22
  98.9 6.4 collective-permute-start.8
  105.3 5.0 collective-permute-start.11
  110.3 11.7 %collective-permute-start.13 = (f32[2,64,512]{1,2,0:T(8,128)}, f32[2,64,512]{1,2,0:T(8,128)}, u32[]{:S(2)}, u32[]{:S(2)}) collective-permute-start(f32[2,64,512]{1,2,0:T(8,128)} %get-tuple-element.727), channel_id=1, source_target_pairs={{16,0},{32,16},{48,32},{64,48},{80,64},{96,80},{112,96},{17,1},{33... | collective-permute-start | bytes 786440 | tf_op jit(solution)/shard_map/ppermute | solution.py:23
  112.4 14.0 %collective-permute-start.17 = (f32[2,128,128]{2,1,0:T(8,128)}, f32[2,128,128]{2,1,0:T(8,128)S(1)}, u32[]{:S(2)}, u32[]{:S(2)}) collective-permute-start(f32[2,128,128]{2,1,0:T(8,128)} %collective-permute-done.16), channel_id=1, source_target_pairs={{16,0},{32,16},{48,32},{64,48},{80,64},{96,80},{112,96},{17,1},{33... | collective-permute-start | bytes 393224 | tf_op jit(solution)/shard_map/ppermute | solution.py:31
  117.8 33.8 %collective-permute-start.25 = (f32[2,128,128]{2,1,0:T(8,128)S(1)}, f32[2,128,128]{2,1,0:T(8,128)S(1)}, u32[]{:S(2)}, u32[]{:S(2)}) collective-permute-start(f32[2,128,128]{2,1,0:T(8,128)S(1)} %broadcast_select_fusion.2), channel_id=1, source_target_pairs={{0,16},{16,32},{32,48},{48,64},{64,80},{80,96},{96,112},{1,17},{17... | collective-permute-start | bytes 393224 | tf_op jit(solution)/shard_map/ppermute | solution.py:31
  122.0 7.0 collective-permute-start.18
  125.1 12.9 %collective-permute-start.23 = (f32[2,128,128]{2,1,0:T(8,128)S(1)}, f32[2,128,128]{2,1,0:T(8,128)S(1)}, u32[]{:S(2)}, u32[]{:S(2)}) collective-permute-start(f32[2,128,128]{2,1,0:T(8,128)S(1)} %broadcast_select_fusion.3), channel_id=1, source_target_pairs={{1,0},{2,1},{3,2},{4,3},{5,4},{6,5},{7,6},{8,7},{9,8},{10,9},{11,1... | collective-permute-start | bytes 393224 | tf_op jit(solution)/shard_map/ppermute | solution.py:31
  126.4 15.5 %collective-permute-start.20 = (f32[2,128,128]{2,1,0:T(8,128)}, f32[2,128,128]{2,1,0:T(8,128)S(1)}, u32[]{:S(2)}, u32[]{:S(2)}) collective-permute-start(f32[2,128,128]{2,1,0:T(8,128)} %collective-permute-done.19), channel_id=1, source_target_pairs={{16,0},{32,16},{48,32},{64,48},{80,64},{96,80},{112,96},{17,1},{33... | collective-permute-start | bytes 393224 | tf_op jit(solution)/shard_map/ppermute | solution.py:31
  129.0 15.7 %collective-permute-start.21 = (f32[2,128,128]{2,1,0:T(8,128)}, f32[2,128,128]{2,1,0:T(8,128)S(1)}, u32[]{:S(2)}, u32[]{:S(2)}) collective-permute-start(f32[2,128,128]{2,1,0:T(8,128)} %broadcast_select_fusion.5), channel_id=1, source_target_pairs={{1,0},{2,1},{3,2},{4,3},{5,4},{6,5},{7,6},{8,7},{9,8},{10,9},{11,1... | collective-permute-start | bytes 393224 | tf_op jit(solution)/shard_map/ppermute | solution.py:31
  131.0 18.1 %collective-permute-start.22 = (f32[2,128,128]{2,1,0:T(8,128)}, f32[2,128,128]{2,1,0:T(8,128)S(1)}, u32[]{:S(2)}, u32[]{:S(2)}) collective-permute-start(f32[2,128,128]{2,1,0:T(8,128)} %broadcast_select_fusion.4), channel_id=1, source_target_pairs={{0,1},{1,2},{2,3},{3,4},{4,5},{5,6},{6,7},{7,8},{8,9},{9,10},{10,1... | collective-permute-start | bytes 393224 | tf_op jit(solution)/shard_map/ppermute | solution.py:31
  138.0 14.3 %collective-permute-start.27 = (f32[2,128,128]{2,1,0:T(8,128)}, f32[2,128,128]{2,1,0:T(8,128)S(1)}, u32[]{:S(2)}, u32[]{:S(2)}) collective-permute-start(f32[2,128,128]{2,1,0:T(8,128)} %collective-permute-done.26), channel_id=1, source_target_pairs={{0,16},{16,32},{32,48},{48,64},{64,80},{80,96},{96,112},{1,17},{17... | collective-permute-start | bytes 393224 | tf_op jit(solution)/shard_map/ppermute | solution.py:31
  141.9 9.1 collective-permute-start.24
  144.7 10.4 collective-permute-start.14
  149.0 11.1 %collective-permute-start.15 = (f32[2,640,64]{1,2,0:T(8,128)S(1)}, f32[2,640,64]{1,2,0:T(8,128)S(1)}, u32[]{:S(2)}, u32[]{:S(2)}) collective-permute-start(f32[2,640,64]{1,2,0:T(8,128)S(1)} %get-tuple-element.725), channel_id=1, source_target_pairs={{1,0},{2,1},{3,2},{4,3},{5,4},{6,5},{7,6},{8,7},{9,8},{10,9},{11,1... | collective-permute-start | bytes 983048 | tf_op jit(solution)/shard_map/ppermute | solution.py:23
  570.5 154.6 %copy-start.3 = (f32[128,128]{1,0:T(8,128)}, f32[128,128]{1,0:T(8,128)S(1)}, u32[]{:S(2)}) copy-start(f32[128,128]{1,0:T(8,128)S(1)} %get-tuple-element.452) | copy-start | bytes 196612
  570.5 154.6 %copy-start.4 = (f32[128,128]{1,0:T(8,128)}, f32[128,128]{1,0:T(8,128)S(1)}, u32[]{:S(2)}) copy-start(f32[128,128]{1,0:T(8,128)S(1)} %get-tuple-element.451) | copy-start | bytes 196612
  570.5 154.6 %copy-start.5 = (f32[128,128]{1,0:T(8,128)}, f32[128,128]{1,0:T(8,128)S(1)}, u32[]{:S(2)}) copy-start(f32[128,128]{1,0:T(8,128)S(1)} %get-tuple-element.450) | copy-start | bytes 196612
  571.6 10.0 collective-permute-start.28
  584.6 137.0 %collective-permute-start.29 = (f32[3,64,640]{2,1,0:T(8,128)S(1)}, f32[3,64,640]{2,1,0:T(8,128)S(1)}, u32[]{:S(2)}, u32[]{:S(2)}) collective-permute-start(f32[3,64,640]{2,1,0:T(8,128)S(1)} %slice.318), channel_id=1, source_target_pairs={{16,0},{32,16},{48,32},{64,48},{80,64},{96,80},{112,96},{17,1},{33... | collective-permute-start | bytes 1474568 | tf_op jit(solution)/shard_map/ppermute | solution.py:31
  725.4 204.4 %collective-permute-start.30 = (f32[3,640,64]{1,2,0:T(8,128)S(1)}, f32[3,640,64]{1,2,0:T(8,128)S(1)}, u32[]{:S(2)}, u32[]{:S(2)}) collective-permute-start(f32[3,640,64]{1,2,0:T(8,128)S(1)} %copy.127), channel_id=1, source_target_pairs={{0,1},{1,2},{2,3},{3,4},{4,5},{5,6},{6,7},{7,8},{8,9},{9,10},{10,1... | collective-permute-start | bytes 1474568 | tf_op jit(solution)/shard_map/ppermute | solution.py:31
  738.5 285.1 %all-reduce.5.cloned.1.call-start = ((), (), s32[]{:S(2)}) async-start(), calls=%async_computation | async-start | bytes 393216 | tf_op jit(solution)/shard_map/psum | solution.py:210
  942.5 83.6 %collective-permute-start.31 = (f32[3,640,64]{1,2,0:T(8,128)S(1)}, f32[3,640,64]{1,2,0:T(8,128)S(1)}, u32[]{:S(2)}, u32[]{:S(2)}) collective-permute-start(f32[3,640,64]{1,2,0:T(8,128)S(1)} %copy.129), channel_id=1, source_target_pairs={{1,0},{2,1},{3,2},{4,3},{5,4},{6,5},{7,6},{8,7},{9,8},{10,9},{11,1... | collective-permute-start | bytes 1474568 | tf_op jit(solution)/shard_map/ppermute | solution.py:31
  1027.3 10.4 copy-start
Sparse Core Ops, SparseCore 0:
  738.6 191.1 all-reduce.6
  933.3 90.2 all-reduce.4
